TPU v7x, 32 devices: a whole 2x2x4 slice. The times are simulated.
32 devices in a mesh: row: 4 (over y, x), col: 8 (over z, core).
Axes of the slice: x: 2, y: 2, z: 4, core: 2. Of those that a mesh axis runs over, the one named last changes fastest.
Arguments:
- features: bfloat16 [32768, 128], P(('row', 'col')), may hold values from -24 to 24
- tile_rows: int32 [4, 8, 1024], P('row', 'col'), may hold values from 0 to 63
- tile_cols: int32 [4, 8, 1024], P('row', 'col'), may hold values from 0 to 31
- edge_lists: int32 [2, 4, 8, 1024, 128], P(None, 'row', 'col'), may hold values from -16 to 127
- tile_counts: int32 [4, 8], P('row', 'col'), may hold values from 128 to 1024, as said below
Outputs:
- hop_one: bfloat16 [32768, 128], P(('row', 'col'))
- hop_two: bfloat16 [32768, 128], P(('row', 'col'))
Inputs may be any that keep to these rules, and one draw needn't show every extreme that they name: `tile_counts`: live tile slots of a block; some block has exactly 1024. `edge_lists`: a negative entry marks an empty edge slot; slots at or past a block's count hold arbitrary entries. `tile_rows`: a tile may occur in several slots; slots at or past a block's count hold arbitrary entries. `tile_cols`: slots at or past a block's count hold arbitrary entries.
All inputs are finite; a program needn't handle non-finite values.
Results may differ from a plain program's by a relative error of at most 0.0058.
Values may be sent and summed in bfloat16 or wider, within the bound.
A program may use at most 192 MiB of HBM per device.

v0:
```python
import jax
import jax.numpy as jnp
from jax import lax
from jax.sharding import PartitionSpec as P

TILE = 128
GROUP = 32


def dense_tiles(dst_ids, src_ids):
    cell_ids = lax.broadcasted_iota(jnp.int32, (1, 1, TILE), 2)
    dst_hot = (dst_ids[:, :, None] == cell_ids).astype(jnp.bfloat16)
    src_hot = (src_ids[:, :, None] == cell_ids).astype(jnp.bfloat16)
    return jnp.einsum("geu,gev->guv", dst_hot, src_hot, preferred_element_type=jnp.float32).astype(
        jnp.bfloat16
    )


def group_turns(live_count):
    return (live_count + GROUP - 1) // GROUP


def alive_mask(start_slot, live_count):
    return (start_slot + lax.iota(jnp.int32, GROUP) < live_count).astype(jnp.float32)


def build_store(row_ids, dst_ids, src_ids, live_count, degree):

    def build_visit(turn_index, state_pair):
        tile_store, partial_degree = state_pair
        start_slot = turn_index * GROUP
        dense_group = dense_tiles(
            lax.dynamic_slice_in_dim(dst_ids, start_slot, GROUP, 0),
            lax.dynamic_slice_in_dim(src_ids, start_slot, GROUP, 0),
        )
        alive = alive_mask(start_slot, live_count)
        row_totals = jnp.sum(dense_group.astype(jnp.float32), axis=2) * alive[:, None]
        group_rows = lax.dynamic_slice_in_dim(row_ids, start_slot, GROUP, 0)
        partial_degree = partial_degree.at[group_rows].add(row_totals)
        tile_store = lax.dynamic_update_slice_in_dim(tile_store, dense_group, start_slot, 0)
        return (tile_store, partial_degree)

    empty = jnp.zeros((row_ids.shape[0], TILE, TILE), jnp.bfloat16)
    return lax.fori_loop(0, group_turns(live_count), build_visit, (empty, degree))


def apply_store(tile_store, row_ids, live_count, fetch, partial_value):

    def apply_visit(turn_index, summed):
        start_slot = turn_index * GROUP
        dense_group = lax.dynamic_slice_in_dim(tile_store, start_slot, GROUP, 0)
        product = jnp.einsum(
            "guv,gvf->guf", dense_group, fetch(start_slot), preferred_element_type=jnp.float32
        )
        alive = alive_mask(start_slot, live_count)
        group_rows = lax.dynamic_slice_in_dim(row_ids, start_slot, GROUP, 0)
        return summed.at[group_rows].add(product * alive[:, None, None])

    return lax.fori_loop(0, group_turns(live_count), apply_visit, partial_value)


def local(features, tile_rows, tile_cols, edge_lists, tile_counts):
    node_count, feat_width = features.shape
    col_size = lax.axis_size("col")
    block_tiles = node_count * col_size // TILE
    rows_own = tile_rows[0, 0]
    cols_own = tile_cols[0, 0]
    dst_own = edge_lists[0, 0, 0]
    src_own = edge_lists[1, 0, 0]
    tile_count = tile_counts[0, 0]
    degree = jnp.zeros((block_tiles, TILE), jnp.float32)
    store_own, degree = build_store(rows_own, dst_own, src_own, tile_count, degree)
    flat_degree = degree.reshape(-1)
    degree_all = lax.psum(flat_degree.astype(jnp.bfloat16), "col").astype(jnp.float32)
    own_degree = lax.dynamic_slice_in_dim(
        degree_all, lax.axis_index("col") * node_count, node_count, 0
    )
    inv_root = lax.rsqrt(1.0 + own_degree)

    def propagate(scaled):
        gathered = lax.all_gather(scaled, "row", axis=0, tiled=True)
        sources = gathered.reshape(-1, TILE, feat_width)

        def fetch_own(start_slot):
            return sources[lax.dynamic_slice_in_dim(cols_own, start_slot, GROUP, 0)]

        partial_value = jnp.zeros((block_tiles, TILE, feat_width), jnp.float32)
        partial_value = apply_store(store_own, rows_own, tile_count, fetch_own, partial_value)
        flat_partial = partial_value.reshape(-1, feat_width)
        return lax.psum_scatter(flat_partial, "col", scatter_dimension=0, tiled=True)

    scaled_zero = (features.astype(jnp.float32) * inv_root[:, None]).astype(jnp.bfloat16)
    first_sum = propagate(scaled_zero)
    hop_one = (first_sum * inv_root[:, None]).astype(jnp.bfloat16)
    scaled_one = (first_sum * (inv_root * inv_root)[:, None]).astype(jnp.bfloat16)
    second_sum = propagate(scaled_one)
    hop_two = (second_sum * inv_root[:, None]).astype(jnp.bfloat16)
    return (hop_one, hop_two)


def solution(mesh):
    placed = (
        P(("row", "col"), None),
        P("row", "col", None),
        P("row", "col", None),
        P(None, "row", "col", None, None),
        P("row", "col"),
    )
    return jax.shard_map(
        local,
        mesh=mesh,
        in_specs=placed,
        out_specs=(P(("row", "col"), None), P(("row", "col"), None)),
        check_vma=False,
    )
```

profile of v0, /device:TPU:4, one launch (start us, length us, event | category | flops | bytes accessed | tf_op | source)
XLA Modules:
  0.0 1095.7 jit_solution(17010022274336452625)
XLA Ops:
  9.2 11.2 %broadcast_in_dim.21.clone = bf16[1024,128,128]{2,1,0:T(8,128)(2,1)} broadcast(bf16[]{:T(256)} %constant.71.clone.1), dimensions={} | broadcast | bytes 33554432 | tf_op jit(solution)/shard_map/broadcast_in_dim | solution.py:43
  20.4 78.1 %while.32 = (s32[]{:T(128)}, bf16[1024,128,128]{2,1,0:T(8,128)(2,1)}, f32[64,128]{1,0:T(8,128)S(1)}, s32[]{:T(128)}, s32[1024,128]{1,0:T(8,128)S(1)}, /*index=5*...) while((s32[]{:T(128)}, ...), condition=%wide.region_3.4_spmd, body=%wide.region_0.3_spmd.sunk | while | flops 136843456 | bytes 5407799 | solution.py:44
  98.6 30.4 %psum.7 = bf16[8192]{0:T(1024)(128)(2,1)S(1)} all-reduce(bf16[8192]{0:T(1024)(128)(2,1)S(1)} %convert_bitcast_fusion), channel_id=1, replica_groups=mesh['row'=4,'col'=8] {'col'}, use_global_device_ids=true, to_apply=%region_4.5 | all-reduce | flops 8192 | bytes 32768 | tf_op jit(solution)/shard_map/psum | solution.py:74
  130.0 105.1 %all-gather.3.cloned.1.call-done = bf16[4096,128]{1,0:T(8,128)(2,1)} async-done(((bf16[1024,128]{1,0:T(8,128)(2,1)}), bf16[4096,128]{1,0:T(8,128)(2,1)}) %all-gather.3.cloned.1.call-update) | async-done | bytes 1048592 | tf_op jit(solution)/shard_map/all_gather | solution.py:81
  237.7 169.7 %while.33 = (s32[]{:T(128)}, f32[64,128,128]{2,1,0:T(8,128)}, s32[]{:T(128)}, s32[1024]{0:T(1024)}, bf16[1024,128,128]{2,1,0:T(8,128)(2,1)}, /*index=5*/s32[1024...) while((s32[]{:T(128)}, f32[64,128,128]{2,1,0:T(8,128)}, ...), condition=%wide.region_7.8_spmd, body=%wide.region_5.7_spmd.sunk | while | flops 135267616 | bytes 12588339 | solution.py:59
  242.7 6.2 scatter_fusion
  254.1 6.3 scatter_fusion
  265.5 6.2 scatter_fusion
  276.8 6.3 scatter_fusion
  288.1 6.3 scatter_fusion
  299.5 6.3 scatter_fusion
  322.2 6.2 scatter_fusion
  333.4 6.2 scatter_fusion
  356.0 6.2 scatter_fusion
  367.2 6.3 scatter_fusion
  389.8 6.2 scatter_fusion
  401.1 6.2 scatter_fusion
  407.4 240.0 %reduce-scatter.3.cloned.1.call-done = f32[1024,128]{1,0:T(8,128)} async-done(((f32[8192,128]{1,0:T(8,128)}), f32[1024,128]{1,0:T(8,128)}) %reduce-scatter.3.cloned.1.call-update) | async-done | bytes 524304 | tf_op jit(solution)/shard_map/reduce_scatter | solution.py:90
  649.7 25.1 %all-gather.5.cloned.1.call-done = bf16[4096,128]{1,0:T(8,128)(2,1)} async-done(((bf16[1024,128]{1,0:T(8,128)(2,1)}), bf16[4096,128]{1,0:T(8,128)(2,1)}) %all-gather.5.cloned.1.call-update) | async-done | bytes 1048592 | tf_op jit(solution)/shard_map/all_gather | solution.py:81
  677.4 169.7 %while.34 = (s32[]{:T(128)}, f32[64,128,128]{2,1,0:T(8,128)}, s32[]{:T(128)}, s32[1024]{0:T(1024)}, bf16[1024,128,128]{2,1,0:T(8,128)(2,1)}, /*index=5*/s32[1024...) while((s32[]{:T(128)}, f32[64,128,128]{2,1,0:T(8,128)}, ...), condition=%wide.region_11.12_spmd, body=%wide.region_9.11_spmd.sunk | while | flops 135267616 | bytes 12588339 | solution.py:59
  682.5 6.2 scatter_fusion.1
  693.8 6.3 scatter_fusion.1
  705.2 6.2 scatter_fusion.1
  716.5 6.3 scatter_fusion.1
  727.9 6.3 scatter_fusion.1
  739.3 6.3 scatter_fusion.1
  761.9 6.2 scatter_fusion.1
  773.2 6.2 scatter_fusion.1
  807.0 6.3 scatter_fusion.1
  829.6 6.2 scatter_fusion.1
  840.9 6.2 scatter_fusion.1
  847.1 240.1 %reduce-scatter.5.cloned.1.call-done = f32[1024,128]{1,0:T(8,128)} async-done(((f32[8192,128]{1,0:T(8,128)}), f32[1024,128]{1,0:T(8,128)}) %reduce-scatter.5.cloned.1.call-update) | async-done | bytes 524304 | tf_op jit(solution)/shard_map/reduce_scatter | solution.py:90
  (281 shorter events, 283.8 us)
Async XLA Ops:
  7.2 227.9 %all-gather.3.cloned.1.call-start = ((), (), s32[]{:S(2)}) async-start(), calls=%async_computation.2 | async-start | bytes 1310720 | tf_op jit(solution)/shard_map/all_gather | solution.py:81
  20.4 108.6 %copy-start = (bf16[1024,128]{1,0:T(8,128)(2,1)S(1)}, bf16[1024,128]{1,0:T(8,128)(2,1)}, u32[]{:S(2)}) copy-start(bf16[1024,128]{1,0:T(8,128)(2,1)} %param.11) | copy-start | bytes 786436
  129.9 517.5 %reduce-scatter.3.cloned.1.call-start = ((), (), s32[]{:S(2)}) async-start(), calls=%async_computation.3 | async-start | bytes 4718592 | tf_op jit(solution)/shard_map/reduce_scatter | solution.py:90
  407.4 267.5 %all-gather.5.cloned.1.call-start = ((), (), s32[]{:S(2)}) async-start(), calls=%async_computation.4 | async-start | bytes 1310720 | tf_op jit(solution)/shard_map/all_gather | solution.py:81
  649.6 437.6 %reduce-scatter.5.cloned.1.call-start = ((), (), s32[]{:S(2)}) async-start(), calls=%async_computation.5 | async-start | bytes 4718592 | tf_op jit(solution)/shard_map/reduce_scatter | solution.py:90
Sparse Core Ops, SparseCore 0:
  130.1 104.9 all-gather.2
  407.5 239.9 reduce-scatter.2
  649.9 24.9 all-gather.4
  847.2 239.9 reduce-scatter.4
where the time goes:
time: 1110 us; the launch traced here: 1100 us
  waiting for transfers between devices  610 us (55%)
  other arithmetic  269 us (24%)
  local copies, waits for them, and re-layouts  103 us (9%)
  matrix products  66.8 us (6%)
  blocking collectives  30.4 us (3%)
  between operations  14.5 us (1%)
    reduce_scatter x2, waiting for transfers between devices, propagate(): lax.psum_scatter(flat_partial, 'col', scatter_dimension=0, tiled=True)  480 us
    scatter-add x30, other arithmetic, apply_visit(): return summed.at[group_rows].add(product * alive[:, None, None])  187 us
    all_gather x2, waiting for transfers between devices, propagate(): gathered = lax.all_gather(scaled, 'row', axis=0, tiled=True)  130 us
    gather x30, local copies, waits for them, and re-layouts, fetch_own(): return sources[lax.dynamic_slice_in_dim(cols_own, start_slot, GROUP, 0)]  59.2 us
    dot_general x30, matrix products, apply_visit(): jnp.einsum('guv,gvf->guf', dense_group, fetch(start_slot), preferred_elem...  49.7 us
    psum x1, blocking collectives, local(): lax.psum(flat_degree.astype(jnp.bfloat16), 'col').astype(jnp.float32)  30.4 us
    convert_element_type x45, other arithmetic, alive_mask(): (start_slot + lax.iota(jnp.int32, GROUP) < live_count).astype(jnp.float32)  29.2 us
    dynamic_update_slice x30, local copies, waits for them, and re-layouts, build_visit(): lax.dynamic_update_slice_in_dim(tile_store, dense_group, start_slot, 0)  26 us
  transfers between devices with their start and end apart: 4, of which 4 were waited for; matrix products, arithmetic and copies ran while one was open for 0% of the time, Pallas kernels for 0%

commit v1 on v0

v1 whole, which is shorter than its diff:
```python
import functools

import jax
import jax.numpy as jnp
from jax import lax
from jax.experimental import pallas as pl
from jax.experimental.pallas import tpu as pltpu
from jax.sharding import PartitionSpec as P

TILE = 128
GROUP = 64
UNROLL = 8
EXTRA = 16
PIECES = 4
CORES = 2
MESH_ID = pl.DeviceIdType.MESH
VMEM_SPEC = pl.BlockSpec(memory_space=pltpu.VMEM)


def live_groups(count_ref):
    first = pl.program_id(0) * GROUP
    live = jnp.clip(count_ref[0] - first, 0, GROUP)
    return first, (live + UNROLL - 1) // UNROLL


def build_kernel(count_ref, rows_ref, dst_ref, src_ref, store_ref, degree_ref, degree_acc):
    @pl.when(pl.program_id(0) == 0)
    def _():
        degree_acc[...] = jnp.zeros_like(degree_acc)

    first, turns = live_groups(count_ref)
    cells = lax.broadcasted_iota(jnp.int32, (TILE, TILE), 0)

    def visit(turn, carry):
        for step in range(UNROLL):
            slot = turn * UNROLL + step
            alive = first + slot < count_ref[0]
            row = jnp.where(alive, rows_ref[first + slot], 0)
            dst = jnp.where(alive, dst_ref[pl.ds(slot, 1), :], -1)
            src = src_ref[pl.ds(slot, 1), :]
            dst_hot = jnp.where(dst == cells, 1.0, 0.0).astype(jnp.bfloat16)
            src_hot = jnp.where(src == cells, 1.0, 0.0).astype(jnp.bfloat16)
            valid = jnp.broadcast_to(jnp.where(src >= 0, 1.0, 0.0), (EXTRA, TILE))
            left = jnp.concatenate([src_hot, valid.astype(jnp.bfloat16)], axis=0)
            both = lax.dot_general(
                left, dst_hot, (((1,), (1,)), ((), ())), preferred_element_type=jnp.float32
            )
            store_ref[slot] = both[:TILE].astype(jnp.bfloat16)
            degree_acc[row] += both[TILE : TILE + 8]
        return carry

    lax.fori_loop(0, turns, visit, 0)

    @pl.when(pl.program_id(0) == pl.num_programs(0) - 1)
    def _():
        degree_ref[...] = degree_acc[:, 0, :]


def apply_kernel(count_ref, rows_ref, cols_ref, store_ref, source_ref, out_ref, acc):
    @pl.when(pl.program_id(0) == 0)
    def _():
        acc[...] = jnp.zeros_like(acc)

    first, turns = live_groups(count_ref)

    def visit(turn, carry):
        products = []
        places = []
        for step in range(UNROLL):
            slot = turn * UNROLL + step
            alive = first + slot < count_ref[0]
            places.append(jnp.where(alive, rows_ref[first + slot], 0))
            col = jnp.where(alive, cols_ref[first + slot], 0)
            product = jnp.dot(
                source_ref[col], store_ref[slot], preferred_element_type=jnp.float32
            )
            acc[places[-1]] += product
        return carry

    lax.fori_loop(0, turns, visit, 0)

    @pl.when(pl.program_id(0) == pl.num_programs(0) - 1)
    def _():
        out_ref[...] = acc[...].astype(jnp.bfloat16)


def greet(targets):
    barrier = pltpu.get_barrier_semaphore()
    for target in targets:
        pl.semaphore_signal(barrier, inc=1, device_id=target, device_id_type=MESH_ID)
    pl.semaphore_wait(barrier, len(targets))


def row_peers(n_row):
    row, col = lax.axis_index("row"), lax.axis_index("col")
    return [(lax.rem(row + d, n_row), col) for d in range(1, n_row)]


def sibling_peers(n_col):
    row, col = lax.axis_index("row"), lax.axis_index("col")
    return [(row, lax.rem(col + CORES * d, n_col)) for d in range(1, n_col // CORES)]


def send(src, dst, send_sem, recv_sem, target):
    copy = pltpu.make_async_remote_copy(
        src_ref=src,
        dst_ref=dst,
        send_sem=send_sem,
        recv_sem=recv_sem,
        device_id=target,
        device_id_type=MESH_ID,
    )
    copy.start()
    return copy


def spread_rows(gathered_ref, start, size, sems, n_row, piece):
    send_sem, recv_sem = sems
    copies = []
    for d, target in enumerate(row_peers(n_row)):
        place = gathered_ref.at[pl.ds(start, size)]
        copies.append(send(place, place, send_sem.at[piece, d], recv_sem.at[piece, d], target))
    return copies


def start_kernel(
    n_row, n_col, part_ref, features_ref, gathered_ref, root_ref, taken, deg_send, deg_recv, row_send, row_recv
):
    row, col = lax.axis_index("row"), lax.axis_index("col")
    own = root_ref.shape[0]
    col_targets = [(row, lax.rem(col + d, n_col)) for d in range(1, n_col)]
    greet(col_targets + row_peers(n_row))
    copies = []
    for d, target in enumerate(col_targets):
        copies.append(
            send(
                part_ref.at[pl.ds(target[1] * own, own)],
                taken.at[d],
                deg_send.at[d],
                deg_recv.at[d],
                target,
            )
        )
    degree = part_ref[pl.ds(pl.multiple_of(col * own, own), own), :]
    for d, copy in enumerate(copies):
        copy.wait_recv()
        degree = degree + taken[d]
    root = lax.rsqrt(1.0 + degree)
    root_ref[...] = root
    size = own // PIECES
    for piece in range(PIECES):
        for tile in range(piece * size, (piece + 1) * size):
            block = features_ref[tile * TILE : (tile + 1) * TILE, :].astype(jnp.float32).T
            gathered_ref[row * own + tile] = (block * root[tile : tile + 1, :]).astype(jnp.bfloat16)
        copies += spread_rows(
            gathered_ref, row * own + piece * size, size, (row_send, row_recv), n_row, piece
        )
    for copy in copies[n_col - 1 :]:
        copy.wait_recv()
    for copy in copies:
        copy.wait_send()


def sum_kernel(n_row, n_col, spread, part_ref, root_ref, *refs):
    if spread:
        hop_ref, gathered_ref, near, staged, far, *sems = refs
        near_send, near_recv, far_send, far_recv, row_send, row_recv = sems
    else:
        hop_ref, near, staged, far, near_send, near_recv, far_send, far_recv = refs
    row, col = lax.axis_index("row"), lax.axis_index("col")
    core = lax.rem(col, CORES)
    chip = col // CORES
    n_chip = n_col // CORES
    partner = (row, chip * CORES + 1 - core)
    siblings = sibling_peers(n_col)
    greet([partner] + siblings + (row_peers(n_row) if spread else []))
    own = root_ref.shape[0]
    size = own // PIECES
    near_copies = {}
    for piece in range(PIECES):
        for d in list(range(1, n_chip)) + [0]:
            other = lax.rem(chip + d, n_chip)
            start = (other * CORES + 1 - core) * own + piece * size
            near_copies[piece, d] = send(
                part_ref.at[pl.ds(start, size)],
                near.at[piece, d],
                near_send.at[piece, d],
                near_recv.at[piece, d],
                partner,
            )
    far_copies = {}
    for piece in range(PIECES):
        for d in range(1, n_chip):
            other = lax.rem(chip + d, n_chip)
            near_copies[piece, d].wait_recv()
            start = (other * CORES + core) * own + piece * size
            staged[piece, d - 1] = (
                part_ref[pl.ds(start, size)].astype(jnp.float32)
                + near[piece, d].astype(jnp.float32)
            ).astype(jnp.bfloat16)
            far_copies[piece, d] = send(
                staged.at[piece, d - 1],
                far.at[piece, d - 1],
                far_send.at[piece, d - 1],
                far_recv.at[piece, d - 1],
                siblings[d - 1],
            )
    row_copies = []
    for piece in range(PIECES):
        near_copies[piece, 0].wait_recv()
        start = (chip * CORES + core) * own + piece * size
        total = part_ref[pl.ds(start, size)].astype(jnp.float32) + near[piece, 0].astype(
            jnp.float32
        )
        for d in range(1, n_chip):
            far_copies[piece, d].wait_recv()
            total = total + far[piece, d - 1].astype(jnp.float32)
        roots = [root_ref[piece * size + tile : piece * size + tile + 1, :] for tile in range(size)]
        if spread:
            for tile in range(size):
                gathered_ref[row * own + piece * size + tile] = (
                    total[tile] * (roots[tile] * roots[tile])
                ).astype(jnp.bfloat16)
            row_copies += spread_rows(
                gathered_ref, row * own + piece * size, size, (row_send, row_recv), n_row, piece
            )
        for tile in range(size):
            place = (piece * size + tile) * TILE
            hop_ref[place : place + TILE, :] = (total[tile] * roots[tile]).T.astype(jnp.bfloat16)
    for copy in row_copies:
        copy.wait_recv()
    for copy in list(near_copies.values()) + list(far_copies.values()) + row_copies:
        copy.wait_send()


def sems(*shape):
    return pltpu.SemaphoreType.DMA(shape)


def comm_params(ident):
    return pltpu.CompilerParams(
        collective_id=ident, has_side_effects=True, vmem_limit_bytes=48 * 2**20
    )


def local(features, tile_rows, tile_cols, edge_lists, tile_counts):
    node_count, feat_width = features.shape
    n_row, n_col = lax.axis_size("row"), lax.axis_size("col")
    own = node_count // TILE
    block_tiles = own * n_col
    source_tiles = own * n_row
    slots = tile_rows.shape[-1]
    rows_own = tile_rows[0, 0]
    cols_own = tile_cols[0, 0]
    count = tile_counts[0]
    bf16, f32 = jnp.bfloat16, jnp.float32

    def last_live(turn, count_ref):
        return jnp.minimum(turn, (jnp.maximum(count_ref[0], 1) - 1) // GROUP)

    store, degree = pl.pallas_call(
        build_kernel,
        grid_spec=pltpu.PrefetchScalarGridSpec(
            num_scalar_prefetch=2,
            grid=(slots // GROUP,),
            in_specs=[
                pl.BlockSpec(
                    (None, None, None, GROUP, TILE),
                    lambda i, n, r, side=side: (side, 0, 0, last_live(i, n), 0),
                )
                for side in range(2)
            ],
            out_specs=[
                pl.BlockSpec((GROUP, TILE, TILE), lambda i, n, r: (last_live(i, n), 0, 0)),
                pl.BlockSpec((block_tiles, TILE), lambda i, n, r: (0, 0)),
            ],
            scratch_shapes=[pltpu.VMEM((block_tiles, 8, TILE), f32)],
        ),
        out_shape=[
            jax.ShapeDtypeStruct((slots, TILE, TILE), bf16),
            jax.ShapeDtypeStruct((block_tiles, TILE), f32),
        ],
        name="build",
    )(count, rows_own, edge_lists, edge_lists)

    gathered_type = jax.ShapeDtypeStruct((source_tiles, feat_width, TILE), bf16)
    gathered, root = pl.pallas_call(
        functools.partial(start_kernel, n_row, n_col),
        out_shape=[gathered_type, jax.ShapeDtypeStruct((own, TILE), f32)],
        in_specs=[VMEM_SPEC] * 2,
        out_specs=[VMEM_SPEC] * 2,
        scratch_shapes=[
            pltpu.VMEM((n_col - 1, own, TILE), f32),
            sems(n_col - 1),
            sems(n_col - 1),
            sems(PIECES, n_row - 1),
            sems(PIECES, n_row - 1),
        ],
        compiler_params=comm_params(0),
        name="start",
    )(degree, features)

    def apply(sources):
        return pl.pallas_call(
            apply_kernel,
            grid_spec=pltpu.PrefetchScalarGridSpec(
                num_scalar_prefetch=3,
                grid=(slots // GROUP,),
                in_specs=[
                    pl.BlockSpec((GROUP, TILE, TILE), lambda i, n, r, c: (last_live(i, n), 0, 0)),
                    pl.BlockSpec((source_tiles, feat_width, TILE), lambda i, n, r, c: (0, 0, 0)),
                ],
                out_specs=pl.BlockSpec((block_tiles, feat_width, TILE), lambda i, n, r, c: (0, 0, 0)),
                scratch_shapes=[pltpu.VMEM((block_tiles, feat_width, TILE), f32)],
            ),
            out_shape=jax.ShapeDtypeStruct((block_tiles, feat_width, TILE), bf16),
            compiler_params=pltpu.CompilerParams(vmem_limit_bytes=48 * 2**20),
            name="apply",
        )(count, rows_own, cols_own, store, sources)

    def collect(part, spread):
        n_chip = n_col // CORES
        size = own // PIECES
        outs = [jax.ShapeDtypeStruct((node_count, feat_width), bf16)]
        semaphores = [sems(PIECES, n_chip)] * 2 + [sems(PIECES, n_chip - 1)] * 2
        if spread:
            outs.append(gathered_type)
            semaphores += [sems(PIECES, n_row - 1)] * 2
        return pl.pallas_call(
            functools.partial(sum_kernel, n_row, n_col, spread),
            out_shape=outs,
            in_specs=[VMEM_SPEC] * 2,
            out_specs=[VMEM_SPEC] * len(outs),
            scratch_shapes=[
                pltpu.VMEM((PIECES, n_chip, size, feat_width, TILE), bf16),
                pltpu.VMEM((PIECES, n_chip - 1, size, feat_width, TILE), bf16),
                pltpu.VMEM((PIECES, n_chip - 1, size, feat_width, TILE), bf16),
            ]
            + semaphores,
            compiler_params=comm_params(1 if spread else 2),
            name="spread" if spread else "finish",
        )(part, root)

    hop_one, gathered = collect(apply(gathered), True)
    (hop_two,) = collect(apply(gathered), False)
    return (hop_one, hop_two)


def solution(mesh):
    placed = (
        P(("row", "col"), None),
        P("row", "col", None),
        P("row", "col", None),
        P(None, "row", "col", None, None),
        P("row", "col"),
    )
    return jax.shard_map(
        local,
        mesh=mesh,
        in_specs=placed,
        out_specs=(P(("row", "col"), None), P(("row", "col"), None)),
        check_vma=False,
    )
```

time: 1110 us -> 188 us (0.17); the launches traced: 1100 us -> 186 us
  waiting for transfers between devices: 610 us -> 0 us
  other arithmetic: 269 us -> 0 us
  Pallas kernels: 0 us -> 183 us
  local copies, waits for them, and re-layouts: 103 us -> 2.18 us
  matrix products: 66.8 us -> 0 us
  blocking collectives: 30.4 us -> 0 us
  between operations: 14.5 us -> 1.4 us
    reduce_scatter x2 -> x0, waiting for transfers between devices: 480 us -> none  [propagate(): lax.psum_scatter(flat_partial, 'col', scatter_dimension=0, tiled=True)]
    scatter-add x45 -> x0, other arithmetic: 199 us -> none  [the longest x30 187 us: apply_visit(): return summed.at[group_rows].add(product * alive[:, None, None])]
    pallas_call x0 -> x6, Pallas kernels: none -> 183 us  [the longest x2 97.4 us: collect(): pl.pallas_call(functools.partial(sum_kernel, n_row, n_col, spread), out_s...]
    all_gather x2 -> x0, waiting for transfers between devices: 130 us -> none  [propagate(): gathered = lax.all_gather(scaled, 'row', axis=0, tiled=True)]
    dot_general x45 -> x0, matrix products: 66.8 us -> none  [the longest x30 49.7 us: apply_visit(): jnp.einsum('guv,gvf->guf', dense_group, fetch(start_slot), preferred_elem...]
    gather x30 -> x0, local copies, waits for them, and re-layouts: 59.2 us -> none  [fetch_own(): return sources[lax.dynamic_slice_in_dim(cols_own, start_slot, GROUP, 0)]]
    select_n x45 -> x0, other arithmetic: 34.7 us -> none  [the longest x30 23.3 us: fetch_own(): return sources[lax.dynamic_slice_in_dim(cols_own, start_slot, GROUP, 0)]]
    convert_element_type x49 -> x0, other arithmetic: 34.3 us -> none  [the longest x45 29.2 us: alive_mask(): (start_slot + lax.iota(jnp.int32, GROUP) < live_count).astype(jnp.float32)]
  transfers between devices with their start and end apart: 4 -> 0, of which waited for: 4 -> 0; matrix products, arithmetic and copies ran while one was open for 0% -> 0% of each run, Pallas kernels for 0% -> 0%
where the time goes in v1:
time: 188 us; the launch traced here: 186 us
  Pallas kernels  183 us (97%)
  local copies, waits for them, and re-layouts  2.18 us (1%)
    pallas_call x2, Pallas kernels, collect(): pl.pallas_call(functools.partial(sum_kernel, n_row, n_col, spread), out_s...  97.4 us
    pallas_call x1, Pallas kernels, local(): pl.pallas_call(functools.partial(start_kernel, n_row, n_col), out_shape=[...  46.7 us
    pallas_call x2, Pallas kernels, apply(): pl.pallas_call(apply_kernel, grid_spec=pltpu.PrefetchScalarGridSpec(num_s...  23.2 us
    pallas_call x1, Pallas kernels, local(): pl.pallas_call(build_kernel, grid_spec=pltpu.PrefetchScalarGridSpec(num_s...  15.5 us

profile of v1, /device:TPU:4, one launch (start us, length us, event | category | flops | bytes accessed | tf_op | source)
XLA Modules:
  0.0 186.4 jit_solution(11945551929317862167)
XLA Ops:
  0.6 0.0 copy-start.3
  0.6 0.0 copy-start.1
  0.7 0.0 copy-start
  1.3 15.5 %build.1 = (bf16[1024,128,128]{2,1,0:T(8,128)(2,1)}, f32[64,128]{1,0:T(8,128)}) custom-call(s32[1]{0:T(128)} %bitcast.3.count_ref, s32[1024]{0:T(1024)} %bitcast.6, s32[2,1,1,1024,128]{4,3,2,1,0:T(8,128)} %src_ref.1, s32[2,1,1,1024,128]{4,3,2,1,0:T(8,128)} %src_ref.1), custom_call_target="tpu_custom_call" | custom-call | tf_op jit(solution)/shard_map/build/pallas_call | solution.py:261
  16.9 0.0 copy-done
  16.9 0.0 copy-start.2
  16.9 0.8 copy-done.2
  17.6 46.7 %start.1 = (bf16[32,128,128]{2,1,0:T(8,128)(2,1)S(1)}, f32[8,128]{1,0:T(8,128)S(1)}) custom-call(f32[64,128]{1,0:T(8,128)S(1)} %copy-done.2, bf16[1024,128]{1,0:T(8,128)(2,1)S(1)} %copy-done), custom_call_target="tpu_custom_call" | custom-call | tf_op jit(solution)/shard_map/start/pallas_call | solution.py:287
  64.4 0.0 copy-done.3
  64.4 0.0 copy-done.1
  64.4 11.3 %apply.2.part_ref = bf16[64,128,128]{2,1,0:T(8,128)(2,1)S(1)} custom-call(s32[1]{0:T(128)} %bitcast.4.count_ref, s32[1024]{0:T(1024)S(1)} %bitcast.7, s32[1024]{0:T(1024)S(1)} %bitcast.9, bf16[1024,128,128]{2,1,0:T(8,128)(2,1)} %get-tuple-element.8.store_ref, bf16[32,128,128]{2,1,0:T(8,128)(2,1)S(1)} %get-tuple-element.10.source_ref), custom_call_target="tpu_custom_call" | custom-call | tf_op jit(solution)/shard_map/apply/pallas_call | solution.py:304
  75.7 49.9 %spread.1 = (bf16[1024,128]{1,0:T(8,128)(2,1)S(1)}, bf16[32,128,128]{2,1,0:T(8,128)(2,1)S(1)}) custom-call(bf16[64,128,128]{2,1,0:T(8,128)(2,1)S(1)} %apply.2.part_ref, f32[8,128]{1,0:T(8,128)S(1)} %get-tuple-element.11.root_ref), custom_call_target="tpu_custom_call" | custom-call | tf_op jit(solution)/shard_map/spread/pallas_call | solution.py:329
  125.6 11.8 %apply.3.part_ref = bf16[64,128,128]{2,1,0:T(8,128)(2,1)S(1)} custom-call(s32[1]{0:T(128)} %bitcast.5.count_ref, s32[1024]{0:T(1024)S(1)} %bitcast.8, s32[1024]{0:T(1024)S(1)} %bitcast.10, bf16[1024,128,128]{2,1,0:T(8,128)(2,1)} %get-tuple-element.8.store_ref, bf16[32,128,128]{2,1,0:T(8,128)(2,1)S(1)} %get-tuple-element.13.source_ref), custom_call_target="tpu_custom_call" | custom-call | tf_op jit(solution)/shard_map/apply/pallas_call | solution.py:304
  137.5 47.5 %finish.1 = bf16[1024,128]{1,0:T(8,128)(2,1)S(1)} custom-call(bf16[64,128,128]{2,1,0:T(8,128)(2,1)S(1)} %apply.3.part_ref, f32[8,128]{1,0:T(8,128)S(1)} %get-tuple-element.11.root_ref), custom_call_target="tpu_custom_call" | custom-call | tf_op jit(solution)/shard_map/finish/pallas_call | solution.py:329
  185.0 0.7 copy.10
  185.7 0.7 copy.11
Async XLA Ops:
  0.6 63.7 %copy-start.3 = (s32[1,1,1024]{2,1,0:T(1,128)S(1)}, s32[1,1,1024]{2,1,0:T(1,128)}, u32[]{:S(2)}) copy-start(s32[1,1,1024]{2,1,0:T(1,128)} %param.7) | copy-start | bytes 12292
  0.6 63.7 %copy-start.1 = (s32[1,1,1024]{2,1,0:T(1,128)S(1)}, s32[1,1,1024]{2,1,0:T(1,128)}, u32[]{:S(2)}) copy-start(s32[1,1,1024]{2,1,0:T(1,128)} %param.6) | copy-start | bytes 12292
  0.7 16.2 %copy-start = (bf16[1024,128]{1,0:T(8,128)(2,1)S(1)}, bf16[1024,128]{1,0:T(8,128)(2,1)}, u32[]{:S(2)}) copy-start(bf16[1024,128]{1,0:T(8,128)(2,1)} %features_ref.1) | copy-start | bytes 786436
  16.9 0.8 copy-start.2
